TPU v7x, 768 devices: a whole 4x8x12 slice. The times are simulated.
768 devices in a mesh: dom: 64 (over y, x, core), sub: 12 (over z).
Axes of the slice: x: 4, y: 8, z: 12, core: 2. Of those that a mesh axis runs over, the one named last changes fastest.
Arguments:
- dof_values: float32 [56, 9, 98304], P(None, None, ('dom', 'sub')), may hold values from -0.6 to 0.6
- stiffness: float32 [3, 56, 56], replicated, may hold values from -0.75 to 0.75
- face_project: float32 [4, 21, 56], replicated, may hold values from -0.75 to 0.75
- face_lift: float32 [4, 56, 21], replicated, may hold values from -1.25 to 1.25
- face_rotate: float32 [3, 21, 21], replicated, may hold values from -1.25 to 1.25
- star_matrices: float32 [3, 9, 9, 98304], P(None, None, None, ('dom', 'sub')), may hold values from -2 to 2
- flux_local: float32 [4, 9, 9, 98304], P(None, None, None, ('dom', 'sub')), may hold values from -1.2 to 1.2
- flux_neighbour: float32 [4, 9, 9, 98304], P(None, None, None, ('dom', 'sub')), may hold values from -1.2 to 1.2
- cluster_labels: int32 [98304], P(('dom', 'sub')), may hold values from 0 to 1, as said below
- neighbour_index: int32 [4, 98304], P(None, ('dom', 'sub')), may hold values from 0 to 351, as said below
- neighbour_face: int32 [4, 98304], P(None, ('dom', 'sub')), may hold values from 0 to 3
- neighbour_orient: int32 [4, 98304], P(None, ('dom', 'sub')), may hold values from 0 to 2
- send_element: int32 [768, 224], P(('dom', 'sub')), may hold values from 0 to 127
- send_face: int32 [768, 224], P(('dom', 'sub')), may hold values from 0 to 3
Outputs:
- new_dofs: float32 [56, 9, 98304], P(None, None, ('dom', 'sub'))
Inputs may be any that keep to these rules, and one draw needn't show every extreme that they name: `cluster_labels`: 0 marks an element of the fine cluster, 1 of the coarse cluster. `neighbour_index`: values below 128 name an own element of the same device; value 128 + s names receive slot s of that device. Every receive slot of a device is named by exactly one face of that device's elements.
All inputs are finite; a program needn't handle non-finite values.
Results may differ from a plain program's by a relative error of at most 0.0001.
Values sent between devices are 32-bit elements; how exact they have to be, the bound alone decides.
A program may use at most 128 MiB of HBM per device.

v0:
```python
import functools

import jax
import jax.numpy as jnp
from jax import lax
from jax.experimental import pallas as pl
from jax.experimental.pallas import tpu as pltpu
from jax.sharding import PartitionSpec as P

MESH = pl.DeviceIdType.MESH
F32, BF16 = jnp.float32, jnp.bfloat16
HIGHEST = lax.Precision.HIGHEST

NB = 56
NBP = 64
NQ = 9
NE = 128
NM = 21
NMP = 24
CURVE = 64
PEER = 8
TERMS = 6
LANES = NQ * NE
TRACE = 224
TRACEP = 256

NN = (((1,), (0,)), ((), ()))
NT = (((1,), (1,)), ((), ()))
TN = (((0,), (0,)), ((), ()))


def mm(a, b, dims=NN):
    return lax.dot_general(a, b, dims, preferred_element_type=F32)


def mm_exact(a, b, dims=NN):
    return lax.dot_general(a, b, dims, precision=HIGHEST, preferred_element_type=F32)


def iota(shape, dim):
    return lax.broadcasted_iota(jnp.int32, shape, dim)


def split(x):
    hi = x.astype(BF16)
    lo = (x - hi.astype(F32)).astype(BF16)
    return hi, lo


def row_block(index):
    out = jnp.zeros_like(index)
    for k in range(1, NQ):
        out = out + (index >= NMP * k).astype(jnp.int32)
    return out


def col(v):
    return slice(v * NE, (v + 1) * NE)


def kernel(
    nd, ns,
    dof_hbm, star_hbm, fluxl_hbm, fluxn_hbm,
    stiff, proj, lift, rot, labels, nidx, nface, norient, selem, sface,
    out,
    dof, star, fluxl, fluxn, starb, fluxlb, fluxnb,
    ader, avol, pst, lst, krc, tall,
    x, i1, i2, xs, z, vol, pi1, pi, t2, t2m, ohs, ohr, oho, zown, zr1, sol, rotm,
    send, recv,
    in_sem, send_sem, recv_sem,
):
    a = lax.axis_index("dom")
    b = lax.axis_index("sub")
    nslots = 2 * CURVE + PEER * ns

    barrier = pltpu.get_barrier_semaphore()

    @pl.when(a > 0)
    def _():
        pl.semaphore_signal(barrier, inc=1, device_id=(a - 1, b), device_id_type=MESH)

    @pl.when(a < nd - 1)
    def _():
        pl.semaphore_signal(barrier, inc=1, device_id=(a + 1, b), device_id_type=MESH)

    for o in range(1, ns):
        pl.semaphore_signal(barrier, inc=1, device_id=(a, lax.rem(b + o, ns)), device_id_type=MESH)

    copies = [
        pltpu.make_async_copy(src, dst, in_sem.at[k])
        for k, (src, dst) in enumerate(
            [(dof_hbm, dof), (star_hbm, star), (fluxl_hbm, fluxl), (fluxn_hbm, fluxn)]
        )
    ]
    for c in copies:
        c.start()

    def stacked(w):
        hi, lo = split(w)
        lane = iota(w.shape, 1)
        return jnp.where(lane < 2 * NBP, hi.astype(F32), lo.astype(F32)).astype(BF16)

    lane = iota((NB, 3 * NBP), 1)
    lane = lane - NBP * ((lane >= NBP).astype(jnp.int32) + (lane >= 2 * NBP).astype(jnp.int32))
    eye3 = (lane == iota((NB, 3 * NBP), 0)).astype(F32)

    def build_map(target, dims):
        tall[...] = jnp.zeros_like(tall)
        for d in range(3):
            tall[d * NB : (d + 1) * NB, :] = mm_exact(stiff[d], eye3, dims)
        target[...] = stacked(tall[0:176, :])

    build_map(ader, TN)
    for f in range(4):
        pi[f * NMP : (f + 1) * NMP, :] = jnp.zeros((NMP, LANES), F32)
        pi[f * NMP : f * NMP + NM, 0:NB] = proj[:, f, :]
    pst[...] = stacked(mm_exact(pi[0:96, 0:NB], eye3))

    ohs[...] = jnp.zeros_like(ohs)
    diagonal = iota((nslots, nslots), 0) == iota((nslots, nslots), 1)
    ones = jnp.ones((nslots, NE), BF16)

    def as_column(row):
        spread = jnp.where(diagonal, jnp.broadcast_to(row.astype(F32), diagonal.shape), 0.0)
        return mm(spread.astype(BF16), ones)

    elem_col = as_column(selem[...])
    face_col = as_column(sface[...])
    lane_e = iota((nslots, NE), 1).astype(F32)
    for f in range(4):
        pick = (elem_col == lane_e) & (face_col == float(f))
        ohs[0:nslots, col(f)] = pick.astype(F32).astype(BF16)

    blank = jnp.zeros((CURVE, TRACEP), F32)
    for ex in range(2):
        @pl.when(a == 0)
        def _():
            recv[ex, 0:CURVE, :] = blank

        @pl.when(a == nd - 1)
        def _():
            recv[ex, CURVE : 2 * CURVE, :] = blank

        recv[ex, nslots:, :] = jnp.zeros((recv.shape[1] - nslots, TRACEP), F32)

    t2[...] = jnp.zeros_like(t2)
    x[NB:, :] = jnp.zeros((NBP - NB, LANES), F32)
    i1[NB:, :] = jnp.zeros((NBP - NB, LANES), F32)
    i2[NB:, :] = jnp.zeros((NBP - NB, LANES), F32)

    copies[0].wait()
    copies[1].wait()
    for v in range(NQ):
        for w in range(NQ):
            for d in range(3):
                starb[v, w, d] = jnp.broadcast_to(star[v, w, d : d + 1, :], (8, NE))

    def load_xs(value):
        hi, lo = split(value)
        xs[0:NBP, :] = hi
        xs[NBP : 2 * NBP, :] = lo
        xs[2 * NBP : 3 * NBP, :] = hi

    def mapped(matrix, target):
        z[...] = mm(matrix[...], xs[...])
        for w0 in range(0, NQ, 3):
            acc = [None, None, None]
            for v in range(NQ):
                for d in range(3):
                    zb = z[d * NB : (d + 1) * NB, col(v)].reshape(NB // 8, 8, NE)
                    for k in range(3):
                        term = zb * starb[v, w0 + k, d][None]
                        acc[k] = term if acc[k] is None else acc[k] + term
            for k in range(3):
                target[0:NB, col(w0 + k)] = acc[k].reshape(NB, NE)

    first_c, second_c = [1.0], [1.0]
    fact = 1.0
    for k in range(1, TERMS):
        fact *= k + 1
        first_c.append(1.0 / fact)
        second_c.append((2.0 ** (k + 1) - 1.0) / fact)

    def coefficient(k, table):
        out_c = jnp.float32(table[-1])
        for j in range(TERMS - 2, 0, -1):
            out_c = jnp.where(k == j, jnp.float32(table[j]), out_c)
        return out_c

    fine_row = labels[...] == 0
    fine = jnp.broadcast_to(fine_row, (NB, NE))

    for v in range(NQ):
        x[0:NB, col(v)] = dof[v]
    i1[...] = x[...]
    i2[...] = x[...]

    def step_one(k, carry):
        load_xs(x[...])
        mapped(ader, x)
        i1[...] = i1[...] + coefficient(k, first_c) * x[...]
        i2[...] = i2[...] + coefficient(k, second_c) * x[...]
        return carry

    lax.fori_loop(1, TERMS, step_one, 0)

    def project(integral):
        load_xs(integral)
        pi[...] = mm(pst[...], xs[...])
        for f in range(4):
            for v in range(NQ):
                t2[v * NMP : (v + 1) * NMP, col(f)] = pi[f * NMP : (f + 1) * NMP, col(v)]
        hi, lo = split(t2[...])
        t2m[0:TRACEP, :] = hi
        t2m[TRACEP:, :] = lo

    def curve_copy(ex, up):
        src = pl.ds(CURVE if up else 0, CURVE)
        dst = pl.ds(0 if up else CURVE, CURVE)
        return pltpu.make_async_remote_copy(
            src_ref=send.at[ex, src, :],
            dst_ref=recv.at[ex, dst, :],
            send_sem=send_sem.at[ex, 0 if up else 1],
            recv_sem=recv_sem.at[ex, 0 if up else 1],
            device_id=(a + 1 if up else a - 1, b),
            device_id_type=MESH,
        )

    def peer_rows(p):
        return pl.ds(pl.multiple_of(2 * CURVE + p * PEER, PEER), PEER)

    def peer_copy(ex, p, source):
        return pltpu.make_async_remote_copy(
            src_ref=send.at[ex, peer_rows(p), :],
            dst_ref=recv.at[ex, peer_rows(source), :],
            send_sem=send_sem.at[ex, 2 + p],
            recv_sem=recv_sem.at[ex, 2 + source],
            device_id=(a, p),
            device_id_type=MESH,
        )

    order = sorted(range(1, ns), key=lambda o: -min(o, ns - o))

    def start_exchange(ex):
        both = mm(ohs[...], t2m[...], NT)
        send[ex] = both[:, 0:TRACEP] + both[:, TRACEP:]
        if ex == 0:
            count = ns - 1 + (a > 0).astype(jnp.int32) + (a < nd - 1).astype(jnp.int32)
            pl.semaphore_wait(barrier, count)
        for o in order:
            p = lax.rem(b + o, ns)
            peer_copy(ex, p, b).start()

        @pl.when(a < nd - 1)
        def _():
            curve_copy(ex, True).start()

        @pl.when(a > 0)
        def _():
            curve_copy(ex, False).start()

        recv[ex, peer_rows(b), :] = send[ex, peer_rows(b), :]

    def finish_exchange(ex):
        @pl.when(a > 0)
        def _():
            curve_copy(ex, True).wait_recv()

        @pl.when(a < nd - 1)
        def _():
            curve_copy(ex, False).wait_recv()

        for o in order:
            p = lax.rem(b + o, ns)
            peer_copy(ex, p, p).wait_recv()

    def finish_sends(ex):
        @pl.when(a < nd - 1)
        def _():
            curve_copy(ex, True).wait_send()

        @pl.when(a > 0)
        def _():
            curve_copy(ex, False).wait_send()

        for o in order:
            p = lax.rem(b + o, ns)
            peer_copy(ex, p, p).wait_send()

    def rotated_own(slot):
        picked = mm(t2m[...], oho[...])
        picked = picked[0:TRACEP, :] + picked[TRACEP:, :]
        hi, lo = split(picked)
        turned = mm(krc[...], jnp.concatenate([hi, lo, hi], axis=0))
        for f in range(4):
            orient = norient[f : f + 1, :]
            pick = jnp.where(
                orient == 0,
                turned[0:TRACE, col(f)],
                jnp.where(orient == 1, turned[TRACE : 2 * TRACE, col(f)], turned[2 * TRACE :, col(f)]),
            )
            if slot == 1:
                pick = pick + jnp.where(fine_row, 0.0, zr1[:, col(f)])
            zown[:, col(f)] = pick

    def local_flux():
        for f in range(4):
            for w0 in range(0, NQ, 3):
                acc = [None, None, None]
                for v in range(NQ):
                    block = pi[f * NMP : (f + 1) * NMP, col(v)].reshape(NMP // 8, 8, NE)
                    for k in range(3):
                        term = block * fluxlb[v, w0 + k, f][None]
                        acc[k] = term if acc[k] is None else acc[k] + term
                for k in range(3):
                    sol[f * NMP : (f + 1) * NMP, col(w0 + k)] = acc[k].reshape(NMP, NE)

    def remote_flux(slot_orient, ex):
        hi, lo = split(recv[ex])
        turned = mm(krc[...], jnp.concatenate([hi, lo, hi], axis=1), NT)
        pick = jnp.where(
            slot_orient < 0.5,
            turned[0:TRACE],
            jnp.where(slot_orient < 1.5, turned[TRACE : 2 * TRACE], turned[2 * TRACE :]),
        )
        hi, lo = split(pick)
        rotm[0:TRACE, :] = hi
        rotm[TRACE:, :] = lo
        arrived = mm(rotm[...], ohr[...])
        zown[...] = zown[...] + arrived[0:TRACE] + arrived[TRACE:]
        for f in range(4):
            for w0 in range(0, NQ, 3):
                acc = [
                    sol[f * NMP : (f + 1) * NMP, col(w0 + k)].reshape(NMP // 8, 8, NE) for k in range(3)
                ]
                for v in range(NQ):
                    block = zown[v * NMP : (v + 1) * NMP, col(f)].reshape(NMP // 8, 8, NE)
                    for k in range(3):
                        acc[k] = acc[k] + block * fluxnb[v, w0 + k, f][None]
                for k in range(3):
                    sol[f * NMP : (f + 1) * NMP, col(w0 + k)] = acc[k].reshape(NMP, NE)
        hi, lo = split(sol[...])
        lifted = mm(lst[...], jnp.concatenate([hi, lo], axis=0))
        vol[...] = vol[...] - lifted[0:NB] - lifted[NBP : NBP + NB]

    project(i1[...])
    start_exchange(0)

    build_map(avol, NN)
    copies[2].wait()
    copies[3].wait()
    for v in range(NQ):
        for w in range(NQ):
            for f in range(4):
                fluxlb[v, w, f] = jnp.broadcast_to(fluxl[v, w, f : f + 1, :], (8, NE))
                fluxnb[v, w, f] = jnp.broadcast_to(fluxn[v, w, f : f + 1, :], (8, NE))

    tall[...] = jnp.zeros_like(tall)
    for f in range(4):
        tall[f * NMP : f * NMP + NM, 0:NB] = lift[:, f, :]
    lane2 = iota((96, 192), 1)
    lane2 = lane2 - 96 * (lane2 >= 96).astype(jnp.int32)
    eye2 = (lane2 == iota((96, 192), 0)).astype(F32)
    wide = mm_exact(tall[0:96, 0:NBP], eye2, TN)
    hi, lo = split(wide)
    lst[0:NBP, :] = hi
    lst[NBP:, :] = lo

    rows = iota((TRACEP, NM), 0)
    tile_of = ((rows - NMP * row_block(rows)) == iota((TRACEP, NM), 1)).astype(F32)
    tile_of = jnp.where(rows < NQ * NMP, tile_of, 0.0)
    same = row_block(iota((TRACE, TRACEP), 0)) == row_block(iota((TRACE, TRACEP), 1))
    for o in range(3):
        turned = mm_exact(tile_of[0:TRACE], rot[o])
        turned = jnp.where(same, mm_exact(turned, tile_of, NT), 0.0)
        hi, lo = split(turned)
        here = slice(o * TRACE, (o + 1) * TRACE)
        krc[here, 0:TRACEP] = hi
        krc[here, TRACEP : 2 * TRACEP] = hi
        krc[here, 2 * TRACEP :] = lo

    nslot_rows = ohr.shape[0]
    for f in range(4):
        index = nidx[f : f + 1, :]
        ohr[:, col(f)] = (iota((nslot_rows, NE), 0) + NE == index).astype(F32).astype(BF16)
        own = jnp.where(index < NE, nface[f : f + 1, :] * NE + index, -1)
        oho[:, col(f)] = (iota((4 * NE, NE), 0) == own).astype(F32).astype(BF16)

    slot_orient = mm(
        jnp.concatenate(
            [jnp.broadcast_to(norient[f : f + 1, :].astype(F32), (16, NE)) for f in range(4)], axis=1
        ).astype(BF16),
        ohr[...],
        NT,
    )[0:1, :]

    rotated_own(0)
    local_flux()
    pi1[...] = pi[...]
    mapped(avol, vol)

    finish_exchange(0)
    remote_flux(slot_orient, 0)
    zr1[...] = zown[...]

    for v in range(NQ):
        x[0:NB, col(v)] = dof[v] + jnp.where(fine, vol[:, col(v)], 0.0)
        dof[v] = x[0:NB, col(v)]
    t = x[...]
    z[0:NBP, :] = t

    def step_two(k, carry):
        load_xs(x[...])
        mapped(ader, x)
        vol[...] = vol[...] + coefficient(k, first_c) * x[0:NB, :]
        return carry

    vol[...] = t[0:NB]
    lax.fori_loop(1, TERMS, step_two, 0)
    for v in range(NQ):
        later = jnp.where(fine, vol[:, col(v)], i2[0:NB, col(v)])
        i1[0:NB, col(v)] = later + jnp.where(fine, 0.0, i1[0:NB, col(v)])
        i2[0:NB, col(v)] = later

    project(i2[...])
    start_exchange(1)

    for v in range(NQ):
        pi[:, col(v)] = pi[:, col(v)] + jnp.where(fine_row, 0.0, pi1[:, col(v)])
    rotated_own(1)
    local_flux()
    load_xs(i1[...])
    mapped(avol, vol)

    finish_exchange(1)
    remote_flux(slot_orient, 1)
    for v in range(NQ):
        out[v] = dof[v] + vol[:, col(v)]
    finish_sends(0)
    finish_sends(1)


def solution(mesh):
    nd, ns = mesh.shape["dom"], mesh.shape["sub"]
    nslots = 2 * CURVE + PEER * ns
    nslots_pad = -(-nslots // 128) * 128

    def per_device(
        dof_values, stiffness, face_project, face_lift, face_rotate, star_matrices,
        flux_local, flux_neighbour, cluster_labels, neighbour_index, neighbour_face,
        neighbour_orient, send_element, send_face,
    ):
        hbm = pl.BlockSpec(memory_space=pl.ANY)
        vmem = pl.BlockSpec(memory_space=pltpu.VMEM)
        scratch = [
            pltpu.VMEM((NQ, NB, NE), F32),
            pltpu.VMEM((NQ, NQ, 3, NE), F32),
            pltpu.VMEM((NQ, NQ, 4, NE), F32),
            pltpu.VMEM((NQ, NQ, 4, NE), F32),
            pltpu.VMEM((NQ, NQ, 3, 8, NE), F32),
            pltpu.VMEM((NQ, NQ, 4, 8, NE), F32),
            pltpu.VMEM((NQ, NQ, 4, 8, NE), F32),
            pltpu.VMEM((176, 3 * NBP), BF16),
            pltpu.VMEM((176, 3 * NBP), BF16),
            pltpu.VMEM((96, 3 * NBP), BF16),
            pltpu.VMEM((2 * NBP, 192), BF16),
            pltpu.VMEM((3 * TRACE, 3 * TRACEP), BF16),
            pltpu.VMEM((176, 3 * NBP), F32),
            pltpu.VMEM((NBP, LANES), F32),
            pltpu.VMEM((NBP, LANES), F32),
            pltpu.VMEM((NBP, LANES), F32),
            pltpu.VMEM((3 * NBP, LANES), BF16),
            pltpu.VMEM((176, LANES), F32),
            pltpu.VMEM((NB, LANES), F32),
            pltpu.VMEM((96, LANES), F32),
            pltpu.VMEM((96, LANES), F32),
            pltpu.VMEM((TRACEP, 4 * NE), F32),
            pltpu.VMEM((2 * TRACEP, 4 * NE), BF16),
            pltpu.VMEM((nslots_pad, 4 * NE), BF16),
            pltpu.VMEM((nslots_pad, 4 * NE), BF16),
            pltpu.VMEM((4 * NE, 4 * NE), BF16),
            pltpu.VMEM((TRACE, 4 * NE), F32),
            pltpu.VMEM((TRACE, 4 * NE), F32),
            pltpu.VMEM((96, LANES), F32),
            pltpu.VMEM((2 * TRACE, nslots_pad), BF16),
            pltpu.VMEM((2, nslots_pad, TRACEP), F32),
            pltpu.VMEM((2, nslots_pad, TRACEP), F32),
            pltpu.SemaphoreType.DMA((4,)),
            pltpu.SemaphoreType.DMA((2, 2 + ns)),
            pltpu.SemaphoreType.DMA((2, 2 + ns)),
        ]
        out = pl.pallas_call(
            functools.partial(kernel, nd, ns),
            out_shape=jax.ShapeDtypeStruct((NQ, NB, NE), F32),
            in_specs=[hbm] * 4 + [vmem] * 10,
            out_specs=vmem,
            scratch_shapes=scratch,
            compiler_params=pltpu.CompilerParams(
                collective_id=0, has_side_effects=True, vmem_limit_bytes=56 * 1024 * 1024
            ),
            name="ader_step",
        )(
            jnp.transpose(dof_values, (1, 0, 2)),
            jnp.transpose(star_matrices, (1, 2, 0, 3)),
            jnp.transpose(flux_local, (1, 2, 0, 3)),
            jnp.transpose(flux_neighbour, (1, 2, 0, 3)),
            stiffness,
            jnp.transpose(face_project, (1, 0, 2)),
            jnp.transpose(face_lift, (2, 0, 1)),
            face_rotate,
            cluster_labels.reshape(1, NE),
            neighbour_index,
            neighbour_face,
            neighbour_orient,
            send_element,
            send_face,
        )
        return jnp.transpose(out, (1, 0, 2))

    both = ("dom", "sub")
    in_specs = (
        P(None, None, both), P(), P(), P(), P(),
        P(None, None, None, both), P(None, None, None, both), P(None, None, None, both),
        P(both), P(None, both), P(None, both), P(None, both), P(both, None), P(both, None),
    )
    return jax.shard_map(
        per_device, mesh=mesh, in_specs=in_specs, out_specs=P(None, None, both), check_vma=False
    )
```

profile of v0, /device:TPU:30, one launch (start us, length us, event | category | flops | bytes accessed | tf_op | source)
XLA Modules:
  0.0 40.6 jit_solution(13923550244673805467)
XLA Ops:
  0.0 38.9 %ader_step.1 = f32[9,56,128]{2,1,0:T(8,128)} custom-call(f32[9,56,128]{2,1,0:T(8,128)} %bitcast.9, f32[9,9,3,128]{3,2,1,0:T(4,128)} %bitcast.10, f32[9,9,4,128]{3,2,1,0:T(4,128)} %bitcast.11, f32[9,9,4,128]{3,2,1,0:T(4,128)} %bitcast.12, f32[3,56,56]{2,1,0:T(8,128)} %stiff.1, f32[21,4,56]{2,1,0:T(4,128)} %bitcast.13, f32[21,4,56]{2,1,0:T(4,128)} %bitcast.14, ...), custom_call_target="tpu_custom_call" | custom-call | tf_op jit(solution)/shard_map/ader_step/pallas_call | solution.py:492
  38.9 1.7 %copy.16 = f32[56,9,128]{2,0,1:T(8,128)} copy(f32[56,9,128]{2,0,1:T(8,128)} %bitcast.8) | data formatting | bytes 516096
where the time goes:
time: 40.8 us; the launch traced here: 40.6 us
  Pallas kernels  38.9 us (95%)
  local copies, waits for them, and re-layouts  1.66 us (4%)
    pallas_call x1, Pallas kernels, per_device(): pl.pallas_call(functools.partial(kernel, nd, ns), out_shape=jax.ShapeDtyp...  38.9 us
    unnamed x1, local copies, waits for them, and re-layouts  1.66 us

commit v1 on v0

--- a/solution.py
+++ b/solution.py
@@ -21,6 +21,7 @@
 PEER = 8
 TERMS = 6
 LANES = NQ * NE
+GROUP = 3
 TRACE = 224
 TRACEP = 256
 
@@ -61,9 +62,12 @@
 def kernel(
     nd, ns,
     dof_hbm, star_hbm, fluxl_hbm, fluxn_hbm,
+    stiff_hbm, proj_hbm, lift_hbm, rot_hbm, labels_hbm, nidx_hbm, nface_hbm, norient_hbm,
+    selem_hbm, sface_hbm,
+    out,
+    dof, star, fluxl, fluxn,
     stiff, proj, lift, rot, labels, nidx, nface, norient, selem, sface,
-    out,
-    dof, star, fluxl, fluxn, starb, fluxlb, fluxnb,
+    starb, fluxlb, fluxnb,
     ader, avol, pst, lst, krc, tall,
     x, i1, i2, xs, z, vol, pi1, pi, t2, t2m, ohs, ohr, oho, zown, zr1, sol, rotm,
     send, recv,
@@ -89,12 +93,23 @@
     copies = [
         pltpu.make_async_copy(src, dst, in_sem.at[k])
         for k, (src, dst) in enumerate(
-            [(dof_hbm, dof), (star_hbm, star), (fluxl_hbm, fluxl), (fluxn_hbm, fluxn)]
+            [
+                (stiff_hbm, stiff), (proj_hbm, proj), (selem_hbm, selem), (sface_hbm, sface),
+                (dof_hbm, dof), (star_hbm, star),
+                (labels_hbm, labels), (lift_hbm, lift), (rot_hbm, rot), (nidx_hbm, nidx),
+                (nface_hbm, nface), (norient_hbm, norient), (fluxl_hbm, fluxl), (fluxn_hbm, fluxn),
+            ]
         )
     ]
     for c in copies:
         c.start()
 
+    ohs[...] = jnp.zeros_like(ohs)
+    t2[...] = jnp.zeros_like(t2)
+    x[NB:, :] = jnp.zeros((NBP - NB, LANES), F32)
+    i1[NB:, :] = jnp.zeros((NBP - NB, LANES), F32)
+    i2[NB:, :] = jnp.zeros((NBP - NB, LANES), F32)
+
     def stacked(w):
         hi, lo = split(w)
         lane = iota(w.shape, 1)
@@ -103,6 +118,9 @@
     lane = iota((NB, 3 * NBP), 1)
     lane = lane - NBP * ((lane >= NBP).astype(jnp.int32) + (lane >= 2 * NBP).astype(jnp.int32))
     eye3 = (lane == iota((NB, 3 * NBP), 0)).astype(F32)
+
+    for c in copies[0:4]:
+        c.wait()
 
     def build_map(target, dims):
         tall[...] = jnp.zeros_like(tall)
@@ -116,7 +134,6 @@
         pi[f * NMP : f * NMP + NM, 0:NB] = proj[:, f, :]
     pst[...] = stacked(mm_exact(pi[0:96, 0:NB], eye3))
 
-    ohs[...] = jnp.zeros_like(ohs)
     diagonal = iota((nslots, nslots), 0) == iota((nslots, nslots), 1)
     ones = jnp.ones((nslots, NE), BF16)
 
@@ -143,13 +160,8 @@
 
         recv[ex, nslots:, :] = jnp.zeros((recv.shape[1] - nslots, TRACEP), F32)
 
-    t2[...] = jnp.zeros_like(t2)
-    x[NB:, :] = jnp.zeros((NBP - NB, LANES), F32)
-    i1[NB:, :] = jnp.zeros((NBP - NB, LANES), F32)
-    i2[NB:, :] = jnp.zeros((NBP - NB, LANES), F32)
-
-    copies[0].wait()
-    copies[1].wait()
+    copies[4].wait()
+    copies[5].wait()
     for v in range(NQ):
         for w in range(NQ):
             for d in range(3):
@@ -162,17 +174,57 @@
         xs[2 * NBP : 3 * NBP, :] = hi
 
     def mapped(matrix, target):
-        z[...] = mm(matrix[...], xs[...])
-        for w0 in range(0, NQ, 3):
-            acc = [None, None, None]
+        z[0] = mm(matrix[...], xs[...])
+
+        def group(g, carry):
+            acc = [None] * GROUP
             for v in range(NQ):
                 for d in range(3):
-                    zb = z[d * NB : (d + 1) * NB, col(v)].reshape(NB // 8, 8, NE)
-                    for k in range(3):
-                        term = zb * starb[v, w0 + k, d][None]
+                    zb = z[0, d * NB : (d + 1) * NB, col(v)].reshape(NB // 8, 8, NE)
+                    for k in range(GROUP):
+                        term = zb * starb[v, g * GROUP + k, d][None]
                         acc[k] = term if acc[k] is None else acc[k] + term
-            for k in range(3):
-                target[0:NB, col(w0 + k)] = acc[k].reshape(NB, NE)
+            for k in range(GROUP):
+                here = pl.ds(pl.multiple_of((g * GROUP + k) * NE, NE), NE)
+                target[0:NB, here] = acc[k].reshape(NB, NE)
+            return carry
+
+        lax.fori_loop(0, NQ // GROUP, group, 0)
+
+    def spread(values):
+        hi, lo = split(values)
+        return mm(ader[...], jnp.concatenate([hi, lo, hi], axis=0))
+
+    def taylor(integrals):
+        wide = GROUP * NE
+        last = NQ - GROUP
+        z[0, :, 0 : last * NE] = spread(x[:, 0 : last * NE])
+
+        def step(t, carry):
+            k = lax.div(t, 3)
+            g = lax.rem(t, 3)
+            behind = pl.ds(pl.multiple_of(lax.rem(g + 2, 3) * wide, NE), wide)
+            now = lax.rem(k, 2)
+            into = lax.rem(k + jnp.minimum(g, 1), 2)
+            made = spread(x[:, behind])
+            acc = [None] * GROUP
+            for v in range(NQ):
+                if v == last:
+                    z[into, :, behind] = made
+                for d in range(3):
+                    zb = z[now, d * NB : (d + 1) * NB, col(v)].reshape(NB // 8, 8, NE)
+                    for j in range(GROUP):
+                        term = zb * starb[v, g * GROUP + j, d][None]
+                        acc[j] = term if acc[j] is None else acc[j] + term
+            for j in range(GROUP):
+                here = pl.ds(pl.multiple_of((g * GROUP + j) * NE, NE), NE)
+                value = acc[j].reshape(NB, NE)
+                x[0:NB, here] = value
+                for ref, table in integrals:
+                    ref[0:NB, here] = ref[0:NB, here] + coefficient(k + 1, table) * value
+            return carry
+
+        lax.fori_loop(0, 3 * (TERMS - 1), step, 0)
 
     first_c, second_c = [1.0], [1.0]
     fact = 1.0
@@ -187,6 +239,7 @@
             out_c = jnp.where(k == j, jnp.float32(table[j]), out_c)
         return out_c
 
+    copies[6].wait()
     fine_row = labels[...] == 0
     fine = jnp.broadcast_to(fine_row, (NB, NE))
 
@@ -195,14 +248,7 @@
     i1[...] = x[...]
     i2[...] = x[...]
 
-    def step_one(k, carry):
-        load_xs(x[...])
-        mapped(ader, x)
-        i1[...] = i1[...] + coefficient(k, first_c) * x[...]
-        i2[...] = i2[...] + coefficient(k, second_c) * x[...]
-        return carry
-
-    lax.fori_loop(1, TERMS, step_one, 0)
+    taylor([(i1, first_c), (i2, second_c)])
 
     def project(integral):
         load_xs(integral)
@@ -347,8 +393,8 @@
     start_exchange(0)
 
     build_map(avol, NN)
-    copies[2].wait()
-    copies[3].wait()
+    for c in copies[7:]:
+        c.wait()
     for v in range(NQ):
         for w in range(NQ):
             for f in range(4):
@@ -406,17 +452,8 @@
     for v in range(NQ):
         x[0:NB, col(v)] = dof[v] + jnp.where(fine, vol[:, col(v)], 0.0)
         dof[v] = x[0:NB, col(v)]
-    t = x[...]
-    z[0:NBP, :] = t
-
-    def step_two(k, carry):
-        load_xs(x[...])
-        mapped(ader, x)
-        vol[...] = vol[...] + coefficient(k, first_c) * x[0:NB, :]
-        return carry
-
-    vol[...] = t[0:NB]
-    lax.fori_loop(1, TERMS, step_two, 0)
+    vol[...] = x[0:NB]
+    taylor([(vol, first_c)])
     for v in range(NQ):
         later = jnp.where(fine, vol[:, col(v)], i2[0:NB, col(v)])
         i1[0:NB, col(v)] = later + jnp.where(fine, 0.0, i1[0:NB, col(v)])
@@ -457,6 +494,16 @@
             pltpu.VMEM((NQ, NQ, 3, NE), F32),
             pltpu.VMEM((NQ, NQ, 4, NE), F32),
             pltpu.VMEM((NQ, NQ, 4, NE), F32),
+            pltpu.VMEM((3, NB, NB), F32),
+            pltpu.VMEM((NM, 4, NB), F32),
+            pltpu.VMEM((NM, 4, NB), F32),
+            pltpu.VMEM((3, NM, NM), F32),
+            pltpu.VMEM((1, NE), jnp.int32),
+            pltpu.VMEM((4, NE), jnp.int32),
+            pltpu.VMEM((4, NE), jnp.int32),
+            pltpu.VMEM((4, NE), jnp.int32),
+            pltpu.VMEM((1, nslots), jnp.int32),
+            pltpu.VMEM((1, nslots), jnp.int32),
             pltpu.VMEM((NQ, NQ, 3, 8, NE), F32),
             pltpu.VMEM((NQ, NQ, 4, 8, NE), F32),
             pltpu.VMEM((NQ, NQ, 4, 8, NE), F32),
@@ -470,7 +517,7 @@
             pltpu.VMEM((NBP, LANES), F32),
             pltpu.VMEM((NBP, LANES), F32),
             pltpu.VMEM((3 * NBP, LANES), BF16),
-            pltpu.VMEM((176, LANES), F32),
+            pltpu.VMEM((2, 176, LANES), F32),
             pltpu.VMEM((NB, LANES), F32),
             pltpu.VMEM((96, LANES), F32),
             pltpu.VMEM((96, LANES), F32),
@@ -485,14 +532,14 @@
             pltpu.VMEM((2 * TRACE, nslots_pad), BF16),
             pltpu.VMEM((2, nslots_pad, TRACEP), F32),
             pltpu.VMEM((2, nslots_pad, TRACEP), F32),
-            pltpu.SemaphoreType.DMA((4,)),
+            pltpu.SemaphoreType.DMA((14,)),
             pltpu.SemaphoreType.DMA((2, 2 + ns)),
             pltpu.SemaphoreType.DMA((2, 2 + ns)),
         ]
         out = pl.pallas_call(
             functools.partial(kernel, nd, ns),
-            out_shape=jax.ShapeDtypeStruct((NQ, NB, NE), F32),
-            in_specs=[hbm] * 4 + [vmem] * 10,
+            out_shape=pltpu.VMEM((NQ, NB, NE), F32),
+            in_specs=[hbm] * 14,
             out_specs=vmem,
             scratch_shapes=scratch,
             compiler_params=pltpu.CompilerParams(

time: 40.8 us -> 40.2 us (0.985)
  local copies, waits for them, and re-layouts: 1.66 us -> 0.7 us
  Pallas kernels: 38.9 us -> 39.4 us
    unnamed x1, local copies, waits for them, and re-layouts: 1.66 us -> 0.7 us
    pallas_call x1, Pallas kernels: 38.9 us -> 39.4 us  [per_device(): pl.pallas_call(functools.partial(kernel, nd, ns), out_shape=pltpu.VMEM((N...]
where the time goes in v1:
time: 40.2 us; the launch traced here: 40.1 us
  Pallas kernels  39.4 us (98%)
  local copies, waits for them, and re-layouts  0.7 us (2%)
    pallas_call x1, Pallas kernels, per_device(): pl.pallas_call(functools.partial(kernel, nd, ns), out_shape=pltpu.VMEM((N...  39.4 us

profile of v1, /device:TPU:30, one launch (start us, length us, event | category | flops | bytes accessed | tf_op | source)
XLA Modules:
  0.0 40.1 jit_solution(10151063422038249349)
XLA Ops:
  0.0 39.4 %ader_step.1 = f32[9,56,128]{2,1,0:T(8,128)S(1)} custom-call(f32[9,56,128]{2,1,0:T(8,128)} %bitcast.9, f32[9,9,3,128]{3,2,1,0:T(4,128)} %bitcast.10, f32[9,9,4,128]{3,2,1,0:T(4,128)} %bitcast.11, f32[9,9,4,128]{3,2,1,0:T(4,128)} %bitcast.12, f32[3,56,56]{2,1,0:T(8,128)} %stiff_hbm.1, f32[21,4,56]{2,1,0:T(4,128)} %bitcast.13, f32[21,4,56]{2,1,0:T(4,128)} %bitcast.14, ...), custom_call_target="tpu_custom_call" | custom-call | tf_op jit(solution)/shard_map/ader_step/pallas_call | solution.py:539
  39.4 0.7 %copy.16 = f32[56,9,128]{2,0,1:T(8,128)} copy(f32[56,9,128]{2,0,1:T(8,128)S(1)} %bitcast.8) | data formatting | bytes 516096

commit v2 on v1

--- a/solution.py
+++ b/solution.py
@@ -110,14 +110,14 @@
     i1[NB:, :] = jnp.zeros((NBP - NB, LANES), F32)
     i2[NB:, :] = jnp.zeros((NBP - NB, LANES), F32)
 
-    def stacked(w):
+    def placed(w, high, low, dims=NN):
         hi, lo = split(w)
-        lane = iota(w.shape, 1)
-        return jnp.where(lane < 2 * NBP, hi.astype(F32), lo.astype(F32)).astype(BF16)
+        return mm(hi.astype(F32), high, dims) + mm(lo.astype(F32), low, dims)
 
     lane = iota((NB, 3 * NBP), 1)
-    lane = lane - NBP * ((lane >= NBP).astype(jnp.int32) + (lane >= 2 * NBP).astype(jnp.int32))
-    eye3 = (lane == iota((NB, 3 * NBP), 0)).astype(F32)
+    row = iota((NB, 3 * NBP), 0)
+    eye_high = ((lane == row) | (lane == row + NBP)).astype(F32)
+    eye_low = (lane == row + 2 * NBP).astype(F32)
 
     for c in copies[0:4]:
         c.wait()
@@ -125,14 +125,14 @@
     def build_map(target, dims):
         tall[...] = jnp.zeros_like(tall)
         for d in range(3):
-            tall[d * NB : (d + 1) * NB, :] = mm_exact(stiff[d], eye3, dims)
-        target[...] = stacked(tall[0:176, :])
+            tall[d * NB : (d + 1) * NB, :] = placed(stiff[d], eye_high, eye_low, dims)
+        target[...] = tall[0:176, :].astype(BF16)
 
     build_map(ader, TN)
     for f in range(4):
         pi[f * NMP : (f + 1) * NMP, :] = jnp.zeros((NMP, LANES), F32)
         pi[f * NMP : f * NMP + NM, 0:NB] = proj[:, f, :]
-    pst[...] = stacked(mm_exact(pi[0:96, 0:NB], eye3))
+    pst[...] = placed(pi[0:96, 0:NB], eye_high, eye_low).astype(BF16)
 
     diagonal = iota((nslots, nslots), 0) == iota((nslots, nslots), 1)
     ones = jnp.ones((nslots, NE), BF16)
@@ -224,7 +224,7 @@
                     ref[0:NB, here] = ref[0:NB, here] + coefficient(k + 1, table) * value
             return carry
 
-        lax.fori_loop(0, 3 * (TERMS - 1), step, 0)
+        lax.fori_loop(0, 3 * (TERMS - 1), step, 0, unroll=5)
 
     first_c, second_c = [1.0], [1.0]
     fact = 1.0

time: 40.2 us -> 39.3 us (0.978)
  the two profiles are of different devices: /device:TPU:30 before, /device:TPU:40 now
where the time goes in v2:
time: 39.3 us; the launch traced here: 39.2 us
  Pallas kernels  38.5 us (98%)
  local copies, waits for them, and re-layouts  0.7 us (2%)
    pallas_call x1, Pallas kernels, per_device(): pl.pallas_call(functools.partial(kernel, nd, ns), out_shape=pltpu.VMEM((N...  38.5 us

profile of v2, /device:TPU:40, one launch (start us, length us, event | category | flops | bytes accessed | tf_op | source)
XLA Modules:
  0.0 39.2 jit_solution(6059023854398868003)
XLA Ops:
  0.0 38.5 %ader_step.1 = f32[9,56,128]{2,1,0:T(8,128)S(1)} custom-call(f32[9,56,128]{2,1,0:T(8,128)} %bitcast.9, f32[9,9,3,128]{3,2,1,0:T(4,128)} %bitcast.10, f32[9,9,4,128]{3,2,1,0:T(4,128)} %bitcast.11, f32[9,9,4,128]{3,2,1,0:T(4,128)} %bitcast.12, f32[3,56,56]{2,1,0:T(8,128)} %stiff_hbm.1, f32[21,4,56]{2,1,0:T(4,128)} %bitcast.13, f32[21,4,56]{2,1,0:T(4,128)} %bitcast.14, ...), custom_call_target="tpu_custom_call" | custom-call | tf_op jit(solution)/shard_map/ader_step/pallas_call | solution.py:539
  38.5 0.7 %copy.16 = f32[56,9,128]{2,0,1:T(8,128)} copy(f32[56,9,128]{2,0,1:T(8,128)S(1)} %bitcast.8) | data formatting | bytes 516096
